TPU v7x, 32 devices: a whole 2x2x4 slice. The times are simulated.
32 devices in a mesh: node: 4 (over y, core), rep: 8 (over z, x).
Axes of the slice: x: 2, y: 2, z: 4, core: 2. Of those that a mesh axis runs over, the one named last changes fastest.
Arguments:
- tokens: bfloat16 [8192, 2048], P(('node', 'rep')), may hold values from -60 to 60
- cotangent: bfloat16 [8192, 512], P(('node', 'rep')), may hold values from -6 to 6
- value_weight: bfloat16 [2048, 512], P('node'), may hold values from -0.25 to 0.25
Outputs:
- input_grad: bfloat16 [8192, 2048], P(('node', 'rep'))
- update: float32 [2048, 512], P('node')
All inputs are finite; a program needn't handle non-finite values.
Results may differ from a plain program's by a relative error of at most 0.025.
Values may be sent and summed in bfloat16 or wider, within the bound.
A program may use at most 64 MiB of HBM per device.

v0:
```python
import math
import jax
import jax.numpy as jnp
from jax import lax
from jax.sharding import PartitionSpec as P

DIN = 2048
HD = 128
NS_ITERS = 5
coef_a = 3.4445
coef_b = -4.775
coef_c = 2.0315
epsilon = 1e-07


def per_device(tokens, cotangent, value_weight):
    width = value_weight.shape[1]
    local_rows = value_weight.shape[0]
    heads = width // HD
    input_grad = lax.dot_general(
        cotangent,
        lax.all_gather(value_weight, "node", axis=0, tiled=True),
        (((1,), (1,)), ((), ())),
        preferred_element_type=jnp.float32,
    ).astype(jnp.bfloat16)
    partial_rows = lax.psum_scatter(
        lax.dot_general(
            tokens, cotangent, (((0,), (0,)), ((), ())), preferred_element_type=jnp.float32
        ).astype(jnp.bfloat16),
        "node",
        scatter_dimension=0,
        tiled=True,
    ).astype(jnp.float32)
    gradient = lax.psum(partial_rows, "rep")
    blocks = gradient.reshape(local_rows, heads, HD)
    local_raw = jnp.einsum("rhi,rhj->hij", blocks, blocks, precision=lax.Precision.HIGHEST)
    gram_raw = lax.psum(local_raw, "node")
    squares = jnp.einsum("hii->h", gram_raw)
    divisor = jnp.sqrt(squares) + epsilon
    start_iterate = blocks / divisor[None, :, None]
    gram = gram_raw / (divisor * divisor)[:, None, None]
    identity = jnp.broadcast_to(jnp.eye(HD, dtype=jnp.float32), (heads, HD, HD))
    total = identity
    for step in range(NS_ITERS):
        factor = (
            coef_a * identity
            + coef_b * gram
            + coef_c * jnp.einsum("hij,hjk->hik", gram, gram, precision=lax.Precision.HIGHEST)
        )
        total = jnp.einsum("hij,hjk->hik", total, factor, precision=lax.Precision.HIGHEST)
        if step + 1 < NS_ITERS:
            halfway = jnp.einsum("hij,hjk->hik", gram, factor, precision=lax.Precision.HIGHEST)
            gram = jnp.einsum("hji,hjk->hik", factor, halfway, precision=lax.Precision.HIGHEST)
    iterate = jnp.einsum("rhi,hij->rhj", start_iterate, total, precision=lax.Precision.HIGHEST)
    update = 0.2 * math.sqrt(DIN) * iterate.reshape(local_rows, width)
    return (input_grad, update)


def solution(mesh):
    in_specs = (P(("node", "rep"), None), P(("node", "rep"), None), P("node", None))
    out_specs = (P(("node", "rep"), None), P("node", None))
    return jax.shard_map(
        per_device, mesh=mesh, in_specs=in_specs, out_specs=out_specs, check_vma=False
    )
```

profile of v0, /device:TPU:0, one launch (start us, length us, event | category | flops | bytes accessed | tf_op | source)
XLA Modules:
  0.0 206.4 jit_solution(13655678280055105823)
XLA Ops:
  7.2 1.2 copy-done
  8.4 3.0 %convolution_convert_fusion = bf16[2048,512]{1,0:T(8,128)(2,1)} fusion(bf16[256,2048]{1,0:T(8,128)(2,1)S(1)} %copy-done, bf16[256,512]{1,0:T(8,128)(2,1)} %param.4), kind=kOutput, calls=%fused_computation | convolution fusion | flops 537919488 | bytes 3407872 | tf_op jit(solution)/shard_map/dot_general | solution.py:27
  11.5 34.0 %reduce-scatter.2.cloned.1.call-done = bf16[512,512]{1,0:T(8,128)(2,1)} async-done(((bf16[2048,512]{1,0:T(8,128)(2,1)}), bf16[512,512]{1,0:T(8,128)(2,1)}) %reduce-scatter.2.cloned.1.call-update) | async-done | bytes 524304 | tf_op jit(solution)/shard_map/reduce_scatter | solution.py:26
  45.5 2.1 %copy_bitcast_fusion = f32[512,4,128]{2,0,1:T(8,128)} fusion(bf16[512,512]{1,0:T(8,128)(2,1)} %reduce-scatter.2.cloned.1.call-done), kind=kLoop, calls=%fused_computation.13 | loop fusion | flops 262144 | bytes 1572864 | tf_op jit(solution)/shard_map/reshape | solution.py:35
  47.7 0.7 all-gather.2.cloned.1.call-update
  48.5 79.5 %all-reduce.3.cloned.1.call-done = f32[512,4,128]{2,0,1:T(8,128)} async-done(((f32[512,4,128]{2,0,1:T(8,128)}), f32[512,4,128]{2,0,1:T(8,128)}) %all-reduce.3.cloned.1.call-update) | async-done | bytes 1048592 | tf_op jit(solution)/shard_map/psum | solution.py:34
  128.0 4.1 %fusion.13 = f32[4,128,128]{2,1,0:T(8,128)} fusion(f32[512,4,128]{2,0,1:T(8,128)} %all-reduce.3.cloned.1.call-done), kind=kOutput, calls=%fused_computation.28 | convolution fusion | flops 402653184 | bytes 1310720 | tf_op jit(solution)/shard_map/rhi,rhj->hij/dot_general | solution.py:36
  132.1 19.6 %all-gather.2.cloned.1.call-done = bf16[2048,512]{1,0:T(8,128)(2,1)} async-done(((bf16[512,512]{1,0:T(8,128)(2,1)}), bf16[2048,512]{1,0:T(8,128)(2,1)}) %all-gather.2.cloned.1.call-update) | async-done | bytes 2097168 | tf_op jit(solution)/shard_map/all_gather | solution.py:22
  151.8 3.3 %convolution_convert_fusion.1 = bf16[256,2048]{1,0:T(8,128)(2,1)} fusion(bf16[256,512]{1,0:T(8,128)(2,1)S(1)} %copy-done.2, bf16[2048,512]{1,0:T(8,128)(2,1)} %all-gather.2.cloned.1.call-done), kind=kOutput, calls=%fused_computation.1 | convolution fusion | flops 537395200 | bytes 3407872 | tf_op jit(solution)/shard_map/dot_general | solution.py:20
  155.1 31.8 %all-reduce.5.cloned.1.call-done = f32[4,128,128]{2,1,0:T(8,128)} async-done(((f32[4,128,128]{2,1,0:T(8,128)}), f32[4,128,128]{2,1,0:T(8,128)}) %all-reduce.5.cloned.1.call-update) | async-done | bytes 262160 | tf_op jit(solution)/shard_map/psum | solution.py:37
  186.8 1.2 select_reduce_fusion
  188.0 1.6 fusion.4
  190.0 0.4 fusion.11
  190.5 0.6 fusion.14
  191.4 0.4 fusion.16
  191.8 0.4 fusion.15
  192.2 0.6 fusion.17
  194.0 0.6 fusion.20
  195.0 0.4 fusion.22
  195.4 0.4 fusion.21
  195.9 0.6 fusion.23
  196.8 0.6 fusion.24
  197.5 1.1 convolution_multiply_fusion
  198.5 1.3 copy.11
  (25 shorter events, 2.9 us)
Async XLA Ops:
  7.2 1.2 copy-start
  7.2 38.4 %reduce-scatter.2.cloned.1.call-start = ((), (), s32[]{:S(2)}) async-start(), calls=%async_computation.2 | async-start | bytes 2621440 | tf_op jit(solution)/shard_map/reduce_scatter | solution.py:26
  11.5 116.6 %all-reduce.3.cloned.1.call-start = ((), (), s32[]{:S(2)}) async-start(), calls=%async_computation.3 | async-start | bytes 2097152 | tf_op jit(solution)/shard_map/psum | solution.py:34
  47.6 104.2 %copy-start.2 = (bf16[256,512]{1,0:T(8,128)(2,1)S(1)}, bf16[256,512]{1,0:T(8,128)(2,1)}, u32[]{:S(2)}) copy-start(bf16[256,512]{1,0:T(8,128)(2,1)} %param.4) | copy-start | bytes 786436
  47.6 104.1 %all-gather.2.cloned.1.call-start = ((), (), s32[]{:S(2)}) async-start(), calls=%async_computation.1 | async-start | bytes 2621440 | tf_op jit(solution)/shard_map/all_gather | solution.py:22
  48.4 138.5 %all-reduce.5.cloned.1.call-start = ((), (), s32[]{:S(2)}) async-start(), calls=%async_computation.4 | async-start | bytes 524288 | tf_op jit(solution)/shard_map/psum | solution.py:37
  186.8 3.2 %copy-start.3 = (f32[4,128,128]{2,1,0:T(8,128)S(1)}, f32[4,128,128]{2,1,0:T(8,128)}, u32[]{:S(2)}) copy-start(f32[4,128,128]{2,1,0:T(8,128)} %all-reduce.5.cloned.1.call-done) | copy-start | bytes 786436
  195.0 2.4 %copy-start.1 = (f32[512,4,128]{2,0,1:T(8,128)S(1)}, f32[512,4,128]{2,0,1:T(8,128)}, u32[]{:S(2)}) copy-start(f32[512,4,128]{2,0,1:T(8,128)} %all-reduce.3.cloned.1.call-done) | copy-start | bytes 3145732
Sparse Core Ops, SparseCore 0:
  11.6 33.9 reduce-scatter.1
  49.6 78.3 all-reduce.2
  129.6 22.1 all-gather.1
  154.5 32.2 all-reduce.4
where the time goes:
time: 207 us; the launch traced here: 206 us
  waiting for transfers between devices  166 us (80%)
  matrix products  20.8 us (10%)
  between operations  14 us (7%)
  other arithmetic  3.28 us (2%)
  local copies, waits for them, and re-layouts  2.5 us (1%)
    psum x1, waiting for transfers between devices, per_device(): gradient = lax.psum(partial_rows, 'rep')  79.5 us
    reduce_scatter x1, waiting for transfers between devices, per_device(): lax.psum_scatter(lax.dot_general(tokens, cotangent, (((0,), (0,)), ((), (...  34 us
    psum x1, waiting for transfers between devices, per_device(): gram_raw = lax.psum(local_raw, 'node')  31.8 us
    all_gather x1, waiting for transfers between devices, per_device(): lax.all_gather(value_weight, 'node', axis=0, tiled=True)  19.6 us
  transfers between devices with their start and end apart: 4, of which 4 were waited for; matrix products, arithmetic and copies ran while one was open for 4% of the time, Pallas kernels for 0%

commit v1 on v0

--- a/solution.py
+++ b/solution.py
@@ -34,7 +34,7 @@
     gradient = lax.psum(partial_rows, "rep")
     blocks = gradient.reshape(local_rows, heads, HD)
     local_raw = jnp.einsum("rhi,rhj->hij", blocks, blocks, precision=lax.Precision.HIGHEST)
-    gram_raw = lax.psum(local_raw, "node")
+    gram_raw = jnp.sum(lax.all_gather(local_raw, "node"), axis=0)
     squares = jnp.einsum("hii->h", gram_raw)
     divisor = jnp.sqrt(squares) + epsilon
     start_iterate = blocks / divisor[None, :, None]

time: 207 us -> 190 us (0.918)
  waiting for transfers between devices: 166 us -> 149 us
    psum x1 -> x0, waiting for transfers between devices: 31.8 us -> none  [per_device(): gram_raw = lax.psum(local_raw, 'node')]
    all_gather x0 -> x1, waiting for transfers between devices: none -> 15.4 us  [per_device(): gram_raw = jnp.sum(lax.all_gather(local_raw, 'node'), axis=0)]
where the time goes in v1:
time: 190 us; the launch traced here: 189 us
  waiting for transfers between devices  149 us (78%)
  matrix products  19.7 us (10%)
  between operations  14 us (7%)
  other arithmetic  3.56 us (2%)
  local copies, waits for them, and re-layouts  2.49 us (1%)
    psum x1, waiting for transfers between devices, per_device(): gradient = lax.psum(partial_rows, 'rep')  79.6 us
    reduce_scatter x1, waiting for transfers between devices, per_device(): lax.psum_scatter(lax.dot_general(tokens, cotangent, (((0,), (0,)), ((), (...  34 us
    all_gather x1, waiting for transfers between devices, per_device(): lax.all_gather(value_weight, 'node', axis=0, tiled=True)  19.6 us
    all_gather x1, waiting for transfers between devices, per_device(): gram_raw = jnp.sum(lax.all_gather(local_raw, 'node'), axis=0)  15.4 us
    dot_general x1, matrix products, per_device(): jnp.einsum('rhi,rhj->hij', blocks, blocks, precision=lax.Precision.HIGHEST)  4.11 us
  transfers between devices with their start and end apart: 4, of which 4 were waited for; matrix products, arithmetic and copies ran while one was open for 4% of the time, Pallas kernels for 0%

profile of v1, /device:TPU:0, one launch (start us, length us, event | category | flops | bytes accessed | tf_op | source)
XLA Modules:
  0.0 189.2 jit_solution(14752643389635039903)
XLA Ops:
  7.2 1.2 copy-done
  8.4 3.0 %convolution_convert_fusion = bf16[2048,512]{1,0:T(8,128)(2,1)} fusion(bf16[256,2048]{1,0:T(8,128)(2,1)S(1)} %copy-done, bf16[256,512]{1,0:T(8,128)(2,1)} %param.4), kind=kOutput, calls=%fused_computation | convolution fusion | flops 537919488 | bytes 3407872 | tf_op jit(solution)/shard_map/dot_general | solution.py:27
  11.5 34.0 %reduce-scatter.2.cloned.1.call-done = bf16[512,512]{1,0:T(8,128)(2,1)} async-done(((bf16[2048,512]{1,0:T(8,128)(2,1)}), bf16[512,512]{1,0:T(8,128)(2,1)}) %reduce-scatter.2.cloned.1.call-update) | async-done | bytes 524304 | tf_op jit(solution)/shard_map/reduce_scatter | solution.py:26
  45.5 2.1 %copy_bitcast_fusion = f32[512,4,128]{2,0,1:T(8,128)} fusion(bf16[512,512]{1,0:T(8,128)(2,1)} %reduce-scatter.2.cloned.1.call-done), kind=kLoop, calls=%fused_computation.13 | loop fusion | flops 262144 | bytes 1572864 | tf_op jit(solution)/shard_map/reshape | solution.py:35
  47.7 0.7 all-gather.4.cloned.1.call-update
  48.4 79.6 %all-reduce.2.cloned.1.call-done = f32[512,4,128]{2,0,1:T(8,128)} async-done(((f32[512,4,128]{2,0,1:T(8,128)}), f32[512,4,128]{2,0,1:T(8,128)}) %all-reduce.2.cloned.1.call-update) | async-done | bytes 1048592 | tf_op jit(solution)/shard_map/psum | solution.py:34
  128.0 4.1 %fusion.13 = f32[4,128,128]{2,1,0:T(8,128)} fusion(f32[512,4,128]{2,0,1:T(8,128)} %all-reduce.2.cloned.1.call-done), kind=kOutput, calls=%fused_computation.28 | convolution fusion | flops 402653184 | bytes 1310720 | tf_op jit(solution)/shard_map/rhi,rhj->hij/dot_general | solution.py:36
  132.2 19.6 %all-gather.4.cloned.1.call-done = bf16[2048,512]{1,0:T(8,128)(2,1)} async-done(((bf16[512,512]{1,0:T(8,128)(2,1)}), bf16[2048,512]{1,0:T(8,128)(2,1)}) %all-gather.4.cloned.1.call-update) | async-done | bytes 2097168 | tf_op jit(solution)/shard_map/all_gather | solution.py:22
  151.8 3.3 %convolution_convert_fusion.1 = bf16[256,2048]{1,0:T(8,128)(2,1)} fusion(bf16[256,512]{1,0:T(8,128)(2,1)S(1)} %copy-done.2, bf16[2048,512]{1,0:T(8,128)(2,1)} %all-gather.4.cloned.1.call-done), kind=kOutput, calls=%fused_computation.1 | convolution fusion | flops 537395200 | bytes 3407872 | tf_op jit(solution)/shard_map/dot_general | solution.py:20
  155.1 15.4 %all-gather.6.cloned.1.call-done = f32[16,128,128]{2,1,0:T(8,128)} async-done(((f32[4,128,128]{2,1,0:T(8,128)}), f32[16,128,128]{2,1,0:T(8,128)}) %all-gather.6.cloned.1.call-update) | async-done | bytes 1048592 | tf_op jit(solution)/shard_map/all_gather | solution.py:37
  170.5 1.3 reduce_sum.18
  171.9 0.5 fusion.4
  172.4 0.4 fusion.11
  173.3 0.6 fusion.14
  174.2 0.4 fusion.16
  175.1 0.6 fusion.17
  176.0 0.4 fusion.19
  176.4 0.4 fusion.18
  176.9 0.6 fusion.20
  178.3 0.4 fusion.21
  178.7 0.6 fusion.23
  179.6 0.6 fusion.24
  180.3 1.1 convolution_multiply_fusion
  181.4 1.3 copy.18
  (24 shorter events, 3.1 us)
Async XLA Ops:
  7.2 1.2 copy-start
  7.2 38.3 %reduce-scatter.2.cloned.1.call-start = ((), (), s32[]{:S(2)}) async-start(), calls=%async_computation.2 | async-start | bytes 2621440 | tf_op jit(solution)/shard_map/reduce_scatter | solution.py:26
  11.4 116.6 %all-reduce.2.cloned.1.call-start = ((), (), s32[]{:S(2)}) async-start(), calls=%async_computation.3 | async-start | bytes 2097152 | tf_op jit(solution)/shard_map/psum | solution.py:34
  47.6 104.2 %copy-start.2 = (bf16[256,512]{1,0:T(8,128)(2,1)S(1)}, bf16[256,512]{1,0:T(8,128)(2,1)}, u32[]{:S(2)}) copy-start(bf16[256,512]{1,0:T(8,128)(2,1)} %param.4) | copy-start | bytes 786436
  47.6 104.1 %all-gather.4.cloned.1.call-start = ((), (), s32[]{:S(2)}) async-start(), calls=%async_computation.1 | async-start | bytes 2621440 | tf_op jit(solution)/shard_map/all_gather | solution.py:22
  48.4 122.1 %all-gather.6.cloned.1.call-start = ((), (), s32[]{:S(2)}) async-start(), calls=%async_computation.4 | async-start | bytes 1310720 | tf_op jit(solution)/shard_map/all_gather | solution.py:37
  177.8 2.4 %copy-start.1 = (f32[512,4,128]{2,0,1:T(8,128)S(1)}, f32[512,4,128]{2,0,1:T(8,128)}, u32[]{:S(2)}) copy-start(f32[512,4,128]{2,0,1:T(8,128)} %all-reduce.2.cloned.1.call-done) | copy-start | bytes 3145732
Sparse Core Ops, SparseCore 0:
  11.6 33.9 reduce-scatter.1
  49.6 78.3 all-reduce.1
  129.6 22.1 all-gather.3
  153.8 16.6 all-gather.5
